TPU v7x, 32 devices: a whole 2x2x4 slice. The times are simulated.
32 devices in a mesh: expert: 4 (over z), shard: 8 (over y, x, core).
Axes of the slice: x: 2, y: 2, z: 4, core: 2. Of those that a mesh axis runs over, the one named last changes fastest.
Arguments:
- master_gate: float32 [64, 2048, 1408], P('expert', 'shard'), may hold values from -0.1875 to 0.1875
- master_up: float32 [64, 2048, 1408], P('expert', 'shard'), may hold values from -0.1875 to 0.1875
- router_weight: float32 [2048, 64], P('shard', 'expert'), may hold values from -0.125 to 0.125
- router_gain: float32 [2048], P('shard'), may hold values from 0.25 to 1.75
Outputs:
- final_gate: bfloat16 [64, 2048, 1408], P('expert', None, 'shard')
- final_up: bfloat16 [64, 2048, 1408], P('expert', None, 'shard')
- scale_gate: float32 [64, 1408], P('expert', 'shard')
- scale_up: float32 [64, 1408], P('expert', 'shard')
- serve_router: bfloat16 [2048, 64], replicated
All inputs are finite; a program needn't handle non-finite values.
Results may differ from a plain program's by a relative error of at most 0.001.
Values may be sent and summed in bfloat16 or wider, within the bound.
A program may use at most 192 MiB of HBM per device.

v0:
```python
import functools

import jax
import jax.numpy as jnp
from jax import lax
from jax.experimental import pallas as pl
from jax.experimental.pallas import tpu as pltpu
from jax.sharding import PartitionSpec as P

GROUP = 8
SLOTS = 16
LANES = 128
VMEM_LIMIT = 62914560


def plain(master_gate, master_up, router_weight, router_gain):
    total_gate, total_up = lax.psum(
        (jnp.sum(master_gate * master_gate, axis=1), jnp.sum(master_up * master_up, axis=1)),
        "shard",
    )
    scale_gate = jnp.sqrt(total_gate)
    scale_up = jnp.sqrt(total_up)
    narrow_gate, narrow_up = (
        (master_gate / jnp.expand_dims(scale_gate, 1)).astype(jnp.bfloat16),
        (master_up / jnp.expand_dims(scale_up, 1)).astype(jnp.bfloat16),
    )
    final_gate, final_up = (
        lax.all_to_all(narrow_gate, "shard", split_axis=2, concat_axis=1, tiled=True),
        lax.all_to_all(narrow_up, "shard", split_axis=2, concat_axis=1, tiled=True),
    )
    scale_gate = lax.dynamic_slice_in_dim(
        scale_gate, lax.axis_index("shard") * final_gate.shape[2], final_gate.shape[2], axis=1
    )
    scale_up = lax.dynamic_slice_in_dim(
        scale_up, lax.axis_index("shard") * final_up.shape[2], final_up.shape[2], axis=1
    )
    part_router = (router_weight * router_gain[:, None]).astype(jnp.bfloat16)
    row_router = lax.all_gather(part_router, "shard", axis=0, tiled=True)
    serve_router = lax.all_gather(row_router, "expert", axis=1, tiled=True)
    return (final_gate, final_up, scale_gate, scale_up, serve_router)


def kernel(n, nz, gate, up, weight, gain, out, scale_out, router_out,
           buf, slots, part, got, inverse, column,
           load_sem, send_sem, own_sem, recv_sem, part_send, part_recv,
           first_send, first_recv, second_send, second_recv, router_own):
    me = lax.axis_index("shard")
    mez = lax.axis_index("expert")
    experts, rows, width = gate.shape
    slabs = 2 * experts
    groups = slabs // GROUP
    narrow = width // n
    router_rows = weight.shape[0]

    def load(source, e, k):
        return pltpu.make_async_copy(source.at[e], buf.at[k], load_sem.at[k])

    def start_gate(e, _):
        load(gate, e, e).start()
        return 0

    def start_up(e, _):
        load(up, e, experts + e).start()
        return 0

    lax.fori_loop(0, experts, start_gate, 0)
    lax.fori_loop(0, experts, start_up, 0)

    barrier = pltpu.get_barrier_semaphore()
    for r in range(1, n):
        pl.semaphore_signal(barrier, inc=1, device_id={"shard": lax.rem(me + r, n)},
                            device_id_type=pl.DeviceIdType.MESH)
    for r in range(1, nz):
        pl.semaphore_signal(barrier, inc=1, device_id={"expert": lax.rem(mez + r, nz)},
                            device_id_type=pl.DeviceIdType.MESH)

    my_rows = pl.ds(pl.multiple_of(mez * router_rows, router_rows), router_rows)
    my_lanes = pl.ds(pl.multiple_of(me * rows, rows), rows)
    column[my_rows, :] = (weight[...] * gain[...]).astype(jnp.bfloat16)
    pl.semaphore_wait(barrier, n - 1 + nz - 1)

    def sums(g):
        def one(i, _):
            k = g * GROUP + i
            load(gate, 0, k).wait()
            x = buf[k]
            part[g, pl.ds(i, 1), :] = jnp.sum(x * x, axis=0, keepdims=True)
            return 0
        lax.fori_loop(0, GROUP, one, 0)

    def part_copy(g, r):
        return pltpu.make_async_remote_copy(
            src_ref=part.at[g], dst_ref=got.at[g, r - 1],
            send_sem=part_send.at[g, r - 1], recv_sem=part_recv.at[g, r - 1],
            device_id={"shard": lax.rem(me + r, n)}, device_id_type=pl.DeviceIdType.MESH)

    def send_part(g):
        for r in range(1, n):
            part_copy(g, r).start()

    def first_copy(r):
        return pltpu.make_async_remote_copy(
            src_ref=column.at[my_rows, :], dst_ref=column.at[my_rows, :],
            send_sem=first_send.at[r - 1], recv_sem=first_recv.at[r - 1],
            device_id={"expert": lax.rem(mez + r, nz)}, device_id_type=pl.DeviceIdType.MESH)

    def second_copy(r):
        return pltpu.make_async_remote_copy(
            src_ref=column, dst_ref=router_out.at[:, my_lanes],
            send_sem=second_send.at[r - 1], recv_sem=second_recv.at[r - 1],
            device_id={"shard": lax.rem(me + r, n)}, device_id_type=pl.DeviceIdType.MESH)

    own_router = pltpu.make_async_copy(column, router_out.at[:, my_lanes], router_own)

    def slab_copy(k, r):
        target = lax.rem(me + r, n)
        s = k % SLOTS
        return pltpu.make_async_remote_copy(
            src_ref=slots.at[s, pl.ds(pl.multiple_of(target * narrow, 16), narrow), :],
            dst_ref=out.at[k, :, my_lanes],
            send_sem=send_sem.at[s, r - 1], recv_sem=recv_sem.at[r - 1],
            device_id={"shard": target}, device_id_type=pl.DeviceIdType.MESH)

    def own_copy(k):
        s = k % SLOTS
        return pltpu.make_async_copy(
            slots.at[s, pl.ds(pl.multiple_of(me * narrow, 16), narrow), :],
            out.at[k, :, my_lanes], own_sem.at[s])

    def send_slab(k):
        for r in range(1, n):
            slab_copy(k, r).start()
        own_copy(k).start()

    def wait_slab(k):
        for r in range(1, n):
            slab_copy(k, r).wait_send()
        own_copy(k).wait()

    def narrow_slab(g, i):
        k = g * GROUP + i

        @pl.when(k >= SLOTS)
        def _():
            wait_slab(k - SLOTS)

        s = k % SLOTS

        def tile(j, _):
            lanes = pl.ds(pl.multiple_of(j * LANES, LANES), LANES)
            y = buf[k, :, lanes] * inverse[j, pl.ds(k, 1), :]
            slots[s, lanes, :] = y.T.astype(jnp.bfloat16)
            return 0

        lax.fori_loop(0, width // LANES, tile, 0)

    for g in range(groups):
        sums(g)
        if g == 0:
            for r in range(1, nz):
                first_copy(r).start()
        else:
            send_part(g - 1)
        if g == 1:
            for r in range(1, nz):
                first_copy(r).wait()
            for r in range(1, n):
                second_copy(r).start()
            own_router.start()

    for g in range(groups):
        for r in range(1, n):
            part_copy(g, r).wait_recv()
        total = part[g]
        for r in range(1, n):
            total = total + got[g, r - 1]
        scale = jnp.sqrt(total)
        scale_out[g * GROUP:(g + 1) * GROUP, :] = scale
        reciprocal = 1.0 / scale
        for j in range(width // LANES):
            inverse[j, g * GROUP:(g + 1) * GROUP, :] = reciprocal[:, j * LANES:(j + 1) * LANES]

        def step(i, _):
            narrow_slab(g, i)
            k = g * GROUP + i

            @pl.when(k > 0)
            def _():
                send_slab(k - 1)

            if g == 0:
                @pl.when(k == 0)
                def _():
                    send_part(groups - 1)
            return 0

        lax.fori_loop(0, GROUP, step, 0)

    for r in range(1, n):
        second_copy(r).wait_send()
    for g in range(groups):
        for r in range(1, n):
            part_copy(g, r).wait_send()
    send_slab(slabs - 1)

    def drain(k, _):
        wait_slab(k)
        return 0

    lax.fori_loop(max(slabs - SLOTS, 0), slabs, drain, 0)
    own_router.wait()
    for r in range(1, n):
        second_copy(r).wait_recv()
        whole = out.at[:, :, my_lanes]
        pltpu.make_async_remote_copy(
            src_ref=whole, dst_ref=whole,
            send_sem=send_sem.at[0, r - 1], recv_sem=recv_sem.at[r - 1],
            device_id={"shard": lax.rem(me + r, n)}, device_id_type=pl.DeviceIdType.MESH,
        ).wait_recv()


def fused(n, nz, master_gate, master_up, router_weight, router_gain):
    experts, rows, width = master_gate.shape
    slabs = 2 * experts
    groups = slabs // GROUP
    narrow = width // n
    router_rows = router_weight.shape[1]
    hbm = pl.BlockSpec(memory_space=pl.ANY)
    vmem = pl.BlockSpec(memory_space=pltpu.VMEM)
    dma = pltpu.SemaphoreType.DMA
    out, scale, router = pl.pallas_call(
        functools.partial(kernel, n, nz),
        out_shape=(
            jax.ShapeDtypeStruct((slabs, narrow, rows * n), jnp.bfloat16),
            jax.ShapeDtypeStruct((slabs, width), jnp.float32),
            jax.ShapeDtypeStruct((router_rows * nz, rows * n), jnp.bfloat16),
        ),
        in_specs=[hbm, hbm, vmem, vmem],
        out_specs=(hbm, vmem, hbm),
        scratch_shapes=[
            pltpu.VMEM((slabs, rows, width), jnp.float32),
            pltpu.VMEM((SLOTS, width, rows), jnp.bfloat16),
            pltpu.VMEM((groups, GROUP, width), jnp.float32),
            pltpu.VMEM((groups, n - 1, GROUP, width), jnp.float32),
            pltpu.VMEM((width // LANES, slabs, LANES), jnp.float32),
            pltpu.VMEM((router_rows * nz, rows), jnp.bfloat16),
            dma((slabs,)), dma((SLOTS, n - 1)), dma((SLOTS,)), dma((n - 1,)),
            dma((groups, n - 1)), dma((groups, n - 1)),
            dma((nz - 1,)), dma((nz - 1,)), dma((n - 1,)), dma((n - 1,)), dma,
        ],
        compiler_params=pltpu.CompilerParams(
            collective_id=0, has_side_effects=True, vmem_limit_bytes=VMEM_LIMIT),
    )(master_gate, master_up, router_weight.T, router_gain[None, :])
    me = lax.axis_index("shard")
    scale = lax.dynamic_slice_in_dim(scale, me * narrow, narrow, axis=1)
    return (
        out[:experts].swapaxes(1, 2), out[experts:].swapaxes(1, 2),
        scale[:experts], scale[experts:], router.T,
    )


def solution(mesh):
    n, nz = mesh.shape["shard"], mesh.shape["expert"]

    def local(master_gate, master_up, router_weight, router_gain):
        experts, rows, width = master_gate.shape
        slabs = 2 * experts
        held = slabs * rows * width * 4 + SLOTS * rows * width * 2 + slabs * (n + 4) * width * 4
        fits = (
            n > 1 and nz > 1 and held <= VMEM_LIMIT and rows % LANES == 0 and width % LANES == 0
            and width % (16 * n) == 0 and slabs % GROUP == 0 and slabs >= 2 * GROUP
            and slabs > SLOTS and router_weight.shape[1] % 16 == 0
        )
        if not fits:
            return plain(master_gate, master_up, router_weight, router_gain)
        return fused(n, nz, master_gate, master_up, router_weight, router_gain)

    in_specs = (
        P("expert", "shard", None),
        P("expert", "shard", None),
        P("shard", "expert"),
        P("shard"),
    )
    out_specs = (
        P("expert", None, "shard"),
        P("expert", None, "shard"),
        P("expert", "shard"),
        P("expert", "shard"),
        P(),
    )
    return jax.shard_map(local, mesh=mesh, in_specs=in_specs, out_specs=out_specs, check_vma=False)
```

profile of v0, /device:TPU:1, one launch (start us, length us, event | category | flops | bytes accessed | tf_op | source)
XLA Modules:
  0.0 300.7 jit_solution(5582569347758330464)
XLA Ops:
  0.6 281.2 %shard_map.83 = (bf16[32,176,2048]{2,1,0:T(8,128)(2,1)}, f32[32,1408]{1,0:T(8,128)}, bf16[64,2048]{1,0:T(8,128)(2,1)}) custom-call(f32[16,256,1408]{2,1,0:T(8,128)} %gate.1, f32[16,256,1408]{2,1,0:T(8,128)} %up.1, f32[16,256]{1,0:T(8,128)} %bitcast.8, f32[1,256]{1,0:T(1,128)} %bitcast.9), custom_call_target="tpu_custom_call" | custom-call | tf_op jit(solution)/shard_map/pallas_call | solution.py:231
  281.9 1.5 fusion
  283.3 0.0 copy-start
  283.3 16.7 %slice_bitcast_fusion = (bf16[16,2048,176]{1,2,0:T(8,128)(2,1)}, bf16[16,2048,176]{1,2,0:T(8,128)(2,1)}) fusion(bf16[32,176,2048]{2,1,0:T(8,128)(2,1)} %get-tuple-element.8), kind=kLoop, calls=%fused_computation | loop fusion | bytes 46137344 | tf_op jit(solution)/shard_map/transpose | solution.py:257
  300.0 0.0 copy-done
  300.0 0.7 copy.10
Async XLA Ops:
  283.3 16.7 %copy-start = (bf16[64,2048]{1,0:T(8,128)(2,1)S(1)}, bf16[64,2048]{1,0:T(8,128)(2,1)}, u32[]{:S(2)}) copy-start(bf16[64,2048]{1,0:T(8,128)(2,1)} %get-tuple-element.10) | copy-start | bytes 786436
where the time goes:
time: 301 us
  Pallas kernels  281 us (93%)
  local copies, waits for them, and re-layouts  18.8 us (6%)
    pallas_call x1, Pallas kernels, fused(): pl.pallas_call(functools.partial(kernel, n, nz), out_shape=(jax.ShapeDtyp...  281 us
    transpose x1, local copies, waits for them, and re-layouts, fused(): out[experts:].swapaxes(1, 2)  16.7 us

commit v1 on v0

v1 whole, which is shorter than its diff:
```python
import functools

import jax
import jax.numpy as jnp
from jax import lax
from jax.experimental import pallas as pl
from jax.experimental.pallas import tpu as pltpu
from jax.sharding import PartitionSpec as P

LANES = 128
FIRST = 3
RING = 6
STREAM = 6
SLOTS = 4
DEPTH = 2
VMEM_LIMIT = 67043328
SPARE = 4194304

def plain(master_gate, master_up, router_weight, router_gain):
    total_gate, total_up = lax.psum(
        (jnp.sum(master_gate * master_gate, axis=1), jnp.sum(master_up * master_up, axis=1)),
        "shard",
    )
    scale_gate = jnp.sqrt(total_gate)
    scale_up = jnp.sqrt(total_up)
    narrow_gate, narrow_up = (
        (master_gate / jnp.expand_dims(scale_gate, 1)).astype(jnp.bfloat16),
        (master_up / jnp.expand_dims(scale_up, 1)).astype(jnp.bfloat16),
    )
    final_gate, final_up = (
        lax.all_to_all(narrow_gate, "shard", split_axis=2, concat_axis=1, tiled=True),
        lax.all_to_all(narrow_up, "shard", split_axis=2, concat_axis=1, tiled=True),
    )
    scale_gate = lax.dynamic_slice_in_dim(
        scale_gate, lax.axis_index("shard") * final_gate.shape[2], final_gate.shape[2], axis=1
    )
    scale_up = lax.dynamic_slice_in_dim(
        scale_up, lax.axis_index("shard") * final_up.shape[2], final_up.shape[2], axis=1
    )
    part_router = (router_weight * router_gain[:, None]).astype(jnp.bfloat16)
    row_router = lax.all_gather(part_router, "shard", axis=0, tiled=True)
    serve_router = lax.all_gather(row_router, "expert", axis=1, tiled=True)
    return (final_gate, final_up, scale_gate, scale_up, serve_router)


def partner(me, n, mask):
    index, bit = 0, 1
    while bit < n:
        mine = lax.rem(me // bit, 2)
        index = index + bit * (1 - mine if mask & bit else mine)
        bit *= 2
    return index


def phases_of(n):
    if n == 8:
        return ((6, 1), (2, 4), (7,), (3, 5))
    return tuple((mask,) for mask in range(1, n))


def stages_of(n):
    doubling = []
    bit = 2
    while bit < n:
        doubling.append((bit,))
        bit *= 2
    return ((tuple(range(2, n, 2)),), tuple(doubling))


def peers_of(stages):
    return sum(len(stage) for stage in stages)


def remote(source, target, send, recv, device):
    return pltpu.make_async_remote_copy(
        src_ref=source, dst_ref=target, send_sem=send, recv_sem=recv,
        device_id=device, device_id_type=pl.DeviceIdType.MESH)


def kernel(n, nz, gate, up, weight, gain, out, scale_gate, scale_up, router_out,
           buf, stream, slots, part0, got0, run0, total0, part1, got1, run1, total1,
           scales, inverse, weight_in, gain_in, piece, column,
           load_sem, stream_sem, router_sem, send_sem, recv_sem, raw_sem,
           send0, recv0, send1, recv1, first_send, first_recv, second_send, second_recv):
    me = lax.axis_index("shard")
    mez = lax.axis_index("expert")
    core = lax.rem(me, 2)
    experts, rows, width = gate.shape
    slabs = 2 * experts
    narrow = width // n
    tiles = width // LANES
    router_rows = weight.shape[0]
    phases = phases_of(n)
    sources = (gate, up)

    def load(src, e):
        k = 2 * e + src
        return pltpu.make_async_copy(sources[src].at[e], buf.at[k % RING], load_sem.at[k % RING])

    def flow(src, e):
        k = (2 * (e - FIRST) + src) % STREAM
        return pltpu.make_async_copy(sources[src].at[e], stream.at[k], stream_sem.at[k])

    for e in range(FIRST):
        for src in range(2):
            load(src, e).start()
    weight_load = pltpu.make_async_copy(weight, weight_in, router_sem.at[0])
    gain_load = pltpu.make_async_copy(gain, gain_in, router_sem.at[1])
    weight_load.start()
    gain_load.start()
    for e in range(FIRST, FIRST + STREAM // 2):
        for src in range(2):
            flow(src, e).start()

    barrier = pltpu.get_barrier_semaphore()
    for mask in range(1, n):
        pl.semaphore_signal(barrier, inc=1, device_id={"shard": partner(me, n, mask)},
                            device_id_type=pl.DeviceIdType.MESH)
    for r in range(1, nz):
        pl.semaphore_signal(barrier, inc=1, device_id={"expert": lax.rem(mez + r, nz)},
                            device_id_type=pl.DeviceIdType.MESH)

    my_lanes = pl.ds(pl.multiple_of(me * rows, rows), rows)
    my_rows = pl.ds(pl.multiple_of(me * narrow, 16), narrow)

    def slab_copy(src, e, mask, raw=False):
        s = (2 * e + src) % SLOTS
        target = partner(me, n, mask)
        return remote(
            slots.at[s, pl.ds(pl.multiple_of(target * narrow, 16), narrow), :],
            out.at[src * experts + e, :, my_lanes],
            send_sem.at[s, mask - 1],
            (raw_sem if raw else recv_sem).at[src, mask - 1],
            {"shard": target})

    def wait_phase(src, e, q, raw=False):
        for mask in phases[q]:
            slab_copy(src, e, mask, raw).wait_send()

    def phase(src, e, q):
        back = q - DEPTH
        before = src
        while back < 0:
            back += len(phases)
            before -= 1
        lag_e = e + before // 2
        if not isinstance(lag_e, int) or lag_e >= 0:
            wait_phase(before % 2, lag_e, back)
        raw = isinstance(e, int) and e == 0
        for mask in phases[q]:
            slab_copy(src, e, mask, raw).start()

    def narrow_slab(src, e, raw=False):
        k = 2 * e + src
        b, s = k % RING, k % SLOTS
        if not isinstance(e, int) or e >= FIRST:
            load(src, e).wait()

        def tile(j, _):
            lanes = pl.ds(pl.multiple_of(j * LANES, LANES), LANES)
            y = buf[b, :, lanes]
            if not raw:
                y = y * inverse[src, j, pl.ds(e, 1), :]
            slots[s, lanes, :] = y.T.astype(jnp.bfloat16)
            return 0

        lax.fori_loop(0, tiles, tile, 0)
        out[src * experts + e, :, my_lanes] = slots[s, my_rows, :]

    def reload(src, e):
        later = e + RING // 2
        if not isinstance(later, int):
            @pl.when(later < experts)
            def _():
                load(src, later).start()
        elif later < experts:
            load(src, later).start()

    def squares(x):
        return jnp.sum(x * x, axis=0, keepdims=True)

    def sums_first(src, e):
        part0[src, e:e + 1, :] = squares(buf[(2 * e + src) % RING])

    def sums_stream(begin, end):
        def one(e, _):
            for src in range(2):
                flow(src, e).wait()
                part1[src, pl.ds(e - FIRST, 1), :] = squares(stream[(2 * (e - FIRST) + src) % STREAM])

                @pl.when(e + STREAM // 2 < experts)
                def _():
                    flow(src, e + STREAM // 2).start()
            return 0
        lax.fori_loop(begin, end, one, 0)

    few, many = stages_of(n)

    def swap(part, got, send, recv):
        return remote(part.at[1 - core], got.at[0], send.at[0], recv.at[0],
                      {"shard": partner(me, n, 1)})

    def passes(stages, s, got, run, send, recv):
        first = 1 + peers_of(stages[:s])
        return [
            remote(run.at[s], got.at[first + i], send.at[first + i], recv.at[first + i],
                   {"shard": partner(me, n, mask)})
            for i, mask in enumerate(stages[s])
        ]

    def share(stages, total, send, recv):
        i = 1 + peers_of(stages)
        return remote(total.at[core], total.at[core], send.at[i], recv.at[i],
                      {"shard": partner(me, n, 1)})

    def swap_end(stages, part, got, run, total, send, recv):
        swap(part, got, send, recv).wait()
        value = part[core] + got[0]
        if stages:
            run[0] = value
        else:
            total[core] = value

    def pass_end(stages, s, got, run, total, send, recv):
        value = run[s]
        for i, copy in enumerate(passes(stages, s, got, run, send, recv)):
            copy.wait()
            value = value + got[1 + peers_of(stages[:s]) + i]
        if s + 1 < len(stages):
            run[s + 1] = value
        else:
            total[core] = value

    def finish(stages, total, begin, end, send, recv):
        share(stages, total, send, recv).wait()
        for src in range(2):
            scale = jnp.sqrt(total[src])
            scales[src, begin:end, :] = scale
            reciprocal = 1.0 / scale
            for j in range(tiles):
                inverse[src, j, begin:end, :] = reciprocal[:, j * LANES:(j + 1) * LANES]

    def mine(x):
        chosen = x[:, :narrow]
        for t in range(1, n):
            chosen = jnp.where(me == t, x[:, t * narrow:(t + 1) * narrow], chosen)
        return chosen

    def first_copy(mask):
        return remote(piece, column.at[:, my_lanes], first_send.at[mask - 1], first_recv.at[mask - 1],
                      {"shard": partner(me, n, mask)})

    my_columns = pl.ds(pl.multiple_of(mez * router_rows, router_rows), router_rows)

    def second_copy(r):
        return remote(column, router_out.at[my_columns, :], second_send.at[r - 1], second_recv.at[r - 1],
                      {"expert": lax.rem(mez + r, nz)})

    def settle(src):
        for mask in range(1, n):
            slab_copy(src, 0, mask, True).wait_recv()
        row = 1.0 / mine(scales[src, 0:1, :])
        pad = -narrow % LANES
        if pad:
            row = jnp.concatenate([row, jnp.zeros((1, pad), jnp.float32)], axis=1)
        factor = jnp.broadcast_to(row, (LANES, narrow + pad)).T[:narrow]

        def tile(j, _):
            lanes = pl.ds(pl.multiple_of(j * LANES, LANES), LANES)
            y = out[src * experts, :, lanes].astype(jnp.float32) * factor
            out[src * experts, :, lanes] = y.astype(jnp.bfloat16)
            return 0

        lax.fori_loop(0, rows * n // LANES, tile, 0)

    last = len(phases) - 1
    half = len(phases) // 2

    load(0, 0).wait()
    narrow_slab(0, 0, raw=True)
    pl.semaphore_wait(barrier, n - 1 + nz - 1)
    for q in range(half):
        phase(0, 0, q)
    sums_first(0, 0)
    for k in range(1, 2 * FIRST):
        load(k % 2, k // 2).wait()
        sums_first(k % 2, k // 2)
    swap(part0, got0, send0, recv0).start()
    reload(0, 0)
    narrow_slab(1, 0, raw=True)
    reload(1, 0)
    swap_end(few, part0, got0, run0, total0, send0, recv0)
    for copy in passes(few, 0, got0, run0, send0, recv0):
        copy.start()

    chunks = [FIRST + (experts - FIRST) * i // 7 for i in range(8)]

    def chunk(i):
        sums_stream(chunks[i], chunks[i + 1])

    def phase_run(k, begin, end):
        for q in range(begin, end):
            phase(k % 2, k // 2, q)

    def ahead(k):
        narrow_slab(k % 2, k // 2)
        reload(k % 2, k // 2)

    phase(0, 0, half)
    weight_load.wait()
    gain_load.wait()
    value = (weight_in[...] * gain_in[...]).astype(jnp.bfloat16)
    piece[...] = value
    column[:, my_lanes] = value
    for mask in range(1, n):
        first_copy(mask).start()
    chunk(0)
    phase_run(0, half + 1, last + 1)
    chunk(1)
    phase(1, 0, 0)
    chunk(2)
    pass_end(few, 0, got0, run0, total0, send0, recv0)
    share(few, total0, send0, recv0).start()
    phase(1, 0, 1)
    chunk(3)
    finish(few, total0, 0, FIRST, send0, recv0)
    phase(1, 0, 2)
    ahead(2)
    phase_run(1, 3, last + 1)
    chunk(4)
    phase(0, 1, 0)
    chunk(5)
    phase(0, 1, 1)
    chunk(6)
    swap(part1, got1, send1, recv1).start()
    ahead(3)
    swap_end(many, part1, got1, run1, total1, send1, recv1)
    for copy in passes(many, 0, got1, run1, send1, recv1):
        copy.start()
    phase_run(2, 2, last + 1)
    phase_run(3, 0, half)
    ahead(4)
    phase_run(3, half, last + 1)
    for s in range(1, len(many)):
        pass_end(many, s - 1, got1, run1, total1, send1, recv1)
        for copy in passes(many, s, got1, run1, send1, recv1):
            copy.start()
    phase_run(4, 0, half)
    ahead(5)
    phase_run(4, half, last + 1)
    for mask in range(1, n):
        first_copy(mask).wait()
    for r in range(1, nz):
        second_copy(r).start()
    router_out[my_columns, :] = column[...]
    pass_end(many, len(many) - 1, got1, run1, total1, send1, recv1)
    share(many, total1, send1, recv1).start()
    phase_run(5, 0, half)
    finish(many, total1, FIRST, experts, send1, recv1)
    ahead(6)
    phase_run(5, half, last + 1)
    for src in range(2):
        settle(src)

    def step(e, _):
        for src in range(2):
            for q in range(half):
                phase(src, e, q)
            if src == 0:
                narrow_slab(1, e)
                reload(1, e)
            else:
                @pl.when(e + 1 < experts)
                def _():
                    narrow_slab(0, e + 1)
                    reload(0, e + 1)
            for q in range(half, last + 1):
                phase(src, e, q)
        return 0

    lax.fori_loop(FIRST, experts, step, 0)

    for ref, src in ((scale_gate, 0), (scale_up, 1)):
        ref[...] = mine(scales[src])
    for r in range(1, nz):
        second_copy(r).wait()
    for q in range(last + 1 - DEPTH, last + 1):
        wait_phase(1, experts - 1, q)
    for mask in range(1, n):
        for src in range(2):
            whole = out.at[src * experts + 1:(src + 1) * experts, :, my_lanes]
            remote(whole, whole, send_sem.at[0, mask - 1], recv_sem.at[src, mask - 1],
                   {"shard": partner(me, n, mask)}).wait_recv()


def deliver(experts, out, scale_gate, scale_up, router,
            to_gate, to_up, to_scale_gate, to_scale_up, to_router, sem):
    copies = [
        pltpu.make_async_copy(source, target, sem.at[i])
        for i, (source, target) in enumerate((
            (out.at[:experts], to_gate), (out.at[experts:], to_up),
            (scale_gate, to_scale_gate), (scale_up, to_scale_up), (router, to_router)))
    ]
    for copy in copies:
        copy.start()
    for copy in copies:
        copy.wait()


def fused(n, nz, master_gate, master_up, router_weight, router_gain):
    experts, rows, width = master_gate.shape
    slabs = 2 * experts
    narrow = width // n
    router_rows = router_weight.shape[1]
    few, many = stages_of(n)
    rest = experts - FIRST
    vmem = pl.BlockSpec(memory_space=pltpu.VMEM)
    hbm = pl.BlockSpec(memory_space=pltpu.HBM)
    dma = pltpu.SemaphoreType.DMA
    f32, bf16 = jnp.float32, jnp.bfloat16

    def sums(count, stages):
        peers = peers_of(stages)
        return [
            pltpu.VMEM((2, count, width), f32),
            pltpu.VMEM((1 + peers, count, width), f32),
            pltpu.VMEM((max(len(stages), 1), count, width), f32),
            pltpu.VMEM((2, count, width), f32),
        ]

    results = pl.pallas_call(
        functools.partial(kernel, n, nz),
        out_shape=(
            pltpu.VMEM((slabs, narrow, rows * n), bf16),
            pltpu.VMEM((experts, narrow), f32),
            pltpu.VMEM((experts, narrow), f32),
            pltpu.VMEM((router_rows * nz, rows * n), bf16),
        ),
        in_specs=[hbm] * 4,
        out_specs=(vmem,) * 4,
        scratch_shapes=[
            pltpu.VMEM((RING, rows, width), f32),
            pltpu.VMEM((STREAM, rows, width), f32),
            pltpu.VMEM((SLOTS, width, rows), bf16),
            *sums(FIRST, few),
            *sums(rest, many),
            pltpu.VMEM((2, experts, width), f32),
            pltpu.VMEM((2, width // LANES, experts, LANES), f32),
            pltpu.VMEM((router_rows, rows), f32),
            pltpu.VMEM((1, rows), f32),
            pltpu.VMEM((router_rows, rows), bf16),
            pltpu.VMEM((router_rows, rows * n), bf16),
            dma((RING,)), dma((STREAM,)), dma((2,)),
            dma((SLOTS, n - 1)), dma((2, n - 1)), dma((2, n - 1)),
            dma((2 + peers_of(few),)), dma((2 + peers_of(few),)),
            dma((2 + peers_of(many),)), dma((2 + peers_of(many),)),
            dma((n - 1,)), dma((n - 1,)), dma((nz - 1,)), dma((nz - 1,)),
        ],
        compiler_params=pltpu.CompilerParams(
            collective_id=0, has_side_effects=True,
            vmem_limit_bytes=VMEM_LIMIT - slabs * narrow * rows * n * 2 - SPARE),
        name="exchange",
    )(master_gate, master_up, router_weight.T, router_gain[None, :])
    final_gate, final_up, scale_gate, scale_up, router = pl.pallas_call(
        functools.partial(deliver, experts),
        out_shape=(
            jax.ShapeDtypeStruct((experts, narrow, rows * n), bf16),
            jax.ShapeDtypeStruct((experts, narrow, rows * n), bf16),
            jax.ShapeDtypeStruct((experts, narrow), f32),
            jax.ShapeDtypeStruct((experts, narrow), f32),
            jax.ShapeDtypeStruct((router_rows * nz, rows * n), bf16),
        ),
        in_specs=[vmem] * 4,
        out_specs=(hbm,) * 5,
        scratch_shapes=[dma((5,))],
        compiler_params=pltpu.CompilerParams(vmem_limit_bytes=1048576),
        name="deliver",
    )(*(pltpu.with_memory_space_constraint(x, pltpu.VMEM) for x in results))
    return (final_gate.swapaxes(1, 2), final_up.swapaxes(1, 2), scale_gate, scale_up, router.T)


def solution(mesh):
    n, nz = mesh.shape["shard"], mesh.shape["expert"]

    def local(master_gate, master_up, router_weight, router_gain):
        experts, rows, width = master_gate.shape
        slabs = 2 * experts
        held = (
            (RING + STREAM) * rows * width * 4 + SLOTS * rows * width * 2
            + slabs * rows * width * 2 + 16 * slabs * width * 4
        )
        fits = (
            n >= 4 and n & (n - 1) == 0 and nz > 1 and held <= VMEM_LIMIT - 2 * SPARE
            and rows % LANES == 0 and width % LANES == 0 and width % (16 * n) == 0
            and experts >= FIRST + 7 and router_weight.shape[1] % 16 == 0
        )
        if not fits:
            return plain(master_gate, master_up, router_weight, router_gain)
        return fused(n, nz, master_gate, master_up, router_weight, router_gain)

    in_specs = (
        P("expert", "shard", None),
        P("expert", "shard", None),
        P("shard", "expert"),
        P("shard"),
    )
    out_specs = (
        P("expert", None, "shard"),
        P("expert", None, "shard"),
        P("expert", "shard"),
        P("expert", "shard"),
        P(),
    )
    return jax.shard_map(local, mesh=mesh, in_specs=in_specs, out_specs=out_specs, check_vma=False)
```

time: 301 us -> 278 us (0.924)
  local copies, waits for them, and re-layouts: 18.8 us -> 0 us
  Pallas kernels: 281 us -> 277 us
    transpose x1 -> x0, local copies, waits for them, and re-layouts: 16.7 us -> none  [fused(): out[experts:].swapaxes(1, 2)]
    pallas_call x1 -> x2, Pallas kernels: 281 us -> 277 us  [the longest x1 269 us: fused(): pl.pallas_call(functools.partial(kernel, n, nz), out_shape=(pltpu.VMEM((s...]
where the time goes in v1:
time: 278 us
  Pallas kernels  277 us (100%)
    pallas_call x1, Pallas kernels, fused(): pl.pallas_call(functools.partial(kernel, n, nz), out_shape=(pltpu.VMEM((s...  269 us
    pallas_call x1, Pallas kernels, fused(): pl.pallas_call(functools.partial(deliver, experts), out_shape=(jax.ShapeD...  8.28 us

profile of v1, /device:TPU:1, one launch (start us, length us, event | category | flops | bytes accessed | tf_op | source)
XLA Modules:
  0.0 277.5 jit_solution(1983240190793132308)
XLA Ops:
  0.6 268.6 %exchange.1 = (bf16[32,176,2048]{2,1,0:T(8,128)(2,1)S(1)}, f32[16,176]{1,0:T(8,128)S(1)}, f32[16,176]{1,0:T(8,128)S(1)}, bf16[64,2048]{1,0:T(8,128)(2,1)S(1)}) custom-call(f32[16,256,1408]{2,1,0:T(8,128)} %gate.1, f32[16,256,1408]{2,1,0:T(8,128)} %up.1, f32[16,256]{1,0:T(8,128)} %bitcast.5, f32[1,256]{1,0:T(1,128)} %bitcast.6), custom_call_target="tpu_custom_call" | custom-call | tf_op jit(solution)/shard_map/exchange/pallas_call | solution.py:431
  269.3 8.3 %deliver.1 = (bf16[16,176,2048]{2,1,0:T(8,128)(2,1)}, bf16[16,176,2048]{2,1,0:T(8,128)(2,1)}, f32[16,176]{1,0:T(8,128)}, f32[16,176]{1,0:T(8,128)}, bf16[64,2048]{1,0:T(8,128)(2,1)}) custom-call(bf16[32,176,2048]{2,1,0:T(8,128)(2,1)S(1)} %get-tuple-element.14.out, f32[16,176]{1,0:T(8,128)S(1)} %get-tuple-element.15.scale_gate, ...), custom_call_target="tpu_custom_call" | custom-call | tf_op jit(solution)/shard_map/deliver/pallas_call | solution.py:464

commit v2 on v1

v2 whole, which is shorter than its diff:
```python
import functools

import jax
import jax.numpy as jnp
from jax import lax
from jax.experimental import pallas as pl
from jax.experimental.pallas import tpu as pltpu
from jax.sharding import PartitionSpec as P

LANES = 128
HELD = 4
STREAM = 6
SLOTS = 4
DEPTH = 3
PHASES = ((6, 1), (2, 4), (7,), (3, 5))
OPENING = (
    ((0, 6, True),),
    ((0, 2, True), (1, 4, True)),
    ((1, 6, True),),
    ((0, 7, False), (0, 1, False)),
    ((0, 3, False), (0, 4, False)),
    ((1, 7, False), (1, 1, False)),
    ((1, 2, False), (1, 5, False)),
    ((1, 3, False), (0, 5, False)),
)
EARLY = ((2, 4, 6),)
LATE = ((2,), (4,))
VMEM_LIMIT = 67043328
SPARE = 4194304

def plain(master_gate, master_up, router_weight, router_gain):
    total_gate, total_up = lax.psum(
        (jnp.sum(master_gate * master_gate, axis=1), jnp.sum(master_up * master_up, axis=1)),
        "shard",
    )
    scale_gate = jnp.sqrt(total_gate)
    scale_up = jnp.sqrt(total_up)
    narrow_gate, narrow_up = (
        (master_gate / jnp.expand_dims(scale_gate, 1)).astype(jnp.bfloat16),
        (master_up / jnp.expand_dims(scale_up, 1)).astype(jnp.bfloat16),
    )
    final_gate, final_up = (
        lax.all_to_all(narrow_gate, "shard", split_axis=2, concat_axis=1, tiled=True),
        lax.all_to_all(narrow_up, "shard", split_axis=2, concat_axis=1, tiled=True),
    )
    scale_gate = lax.dynamic_slice_in_dim(
        scale_gate, lax.axis_index("shard") * final_gate.shape[2], final_gate.shape[2], axis=1
    )
    scale_up = lax.dynamic_slice_in_dim(
        scale_up, lax.axis_index("shard") * final_up.shape[2], final_up.shape[2], axis=1
    )
    part_router = (router_weight * router_gain[:, None]).astype(jnp.bfloat16)
    row_router = lax.all_gather(part_router, "shard", axis=0, tiled=True)
    serve_router = lax.all_gather(row_router, "expert", axis=1, tiled=True)
    return (final_gate, final_up, scale_gate, scale_up, serve_router)


def partner(me, n, mask):
    index, bit = 0, 1
    while bit < n:
        mine = lax.rem(me // bit, 2)
        index = index + bit * (1 - mine if mask & bit else mine)
        bit *= 2
    return index


def peers_of(stages):
    return sum(len(stage) for stage in stages)


def remote(source, target, send, recv, device):
    return pltpu.make_async_remote_copy(
        src_ref=source, dst_ref=target, send_sem=send, recv_sem=recv,
        device_id=device, device_id_type=pl.DeviceIdType.MESH)


def kernel(n, nz, gate, up, weight, gain, out, scale_gate, scale_up, router_out,
           buf, stream, slots, part0, got0, part1, got1, run1, total1, part2, got2, run2, total2,
           scales, inverse, weight_in, gain_in, piece, column,
           load_sem, stream_sem, router_sem, send_sem, recv_sem, raw_sem,
           send0, recv0, send1, recv1, send2, recv2,
           first_send, first_recv, second_send, second_recv):
    me = lax.axis_index("shard")
    mez = lax.axis_index("expert")
    core = lax.rem(me, 2)
    experts, rows, width = gate.shape
    narrow = width // n
    tiles = width // LANES
    router_rows = weight.shape[0]
    sources = (gate, up)
    ring = 2 * HELD

    def load(src, e):
        k = (2 * e + src) % ring
        return pltpu.make_async_copy(sources[src].at[e], buf.at[k], load_sem.at[k])

    def flow(src, e):
        k = (2 * (e - HELD) + src) % STREAM
        return pltpu.make_async_copy(sources[src].at[e], stream.at[k], stream_sem.at[k])

    for e in range(HELD):
        for src in range(2):
            load(src, e).start()
    weight_load = pltpu.make_async_copy(weight, weight_in, router_sem.at[0])
    gain_load = pltpu.make_async_copy(gain, gain_in, router_sem.at[1])
    weight_load.start()
    gain_load.start()
    for e in range(HELD, HELD + STREAM // 2):
        for src in range(2):
            flow(src, e).start()

    barrier = pltpu.get_barrier_semaphore()
    for mask in range(1, n):
        pl.semaphore_signal(barrier, inc=1, device_id={"shard": partner(me, n, mask)},
                            device_id_type=pl.DeviceIdType.MESH)
    for r in range(1, nz):
        pl.semaphore_signal(barrier, inc=1, device_id={"expert": lax.rem(mez + r, nz)},
                            device_id_type=pl.DeviceIdType.MESH)

    my_lanes = pl.ds(pl.multiple_of(me * rows, rows), rows)
    my_rows = pl.ds(pl.multiple_of(me * narrow, 16), narrow)

    def slab_copy(src, e, mask, raw):
        s = 2 + src if raw else (2 * e + src) % SLOTS
        target = partner(me, n, mask)
        return remote(
            slots.at[s, pl.ds(pl.multiple_of(target * narrow, 16), narrow), :],
            out.at[src * experts + e, :, my_lanes],
            send_sem.at[s, mask - 1], (raw_sem if raw else recv_sem).at[src, mask - 1],
            {"shard": target})

    def units(src, e, q):
        if isinstance(e, int) and e == 0:
            return OPENING[len(PHASES) * src + q]
        return [(src, mask, False) for mask in PHASES[q]]

    def wait_phase(src, e, q):
        for which, mask, raw in units(src, e, q):
            slab_copy(which, e, mask, raw).wait_send()

    def phase(src, e, q):
        back, before = q - DEPTH, src
        while back < 0:
            back += len(PHASES)
            before -= 1
        lag = e + before // 2
        if not isinstance(lag, int) or lag >= 0:
            wait_phase(before % 2, lag, back)
        for which, mask, raw in units(src, e, q):
            slab_copy(which, e, mask, raw).start()

    def raw_block(src, mask):
        begin = partner(me, n, mask) * narrow

        def tile(j, _):
            lanes = pl.ds(pl.multiple_of(j * LANES, LANES), LANES)
            slots[2 + src, lanes, :] = buf[src, :, lanes].T.astype(jnp.bfloat16)
            return 0

        lax.fori_loop(begin // LANES, (begin + narrow - 1) // LANES + 1, tile, 0)

    def narrow_slab(src, e):
        k = 2 * e + src
        b, s = k % ring, k % SLOTS
        if not isinstance(e, int) or e >= HELD:
            load(src, e).wait()

        def tile(j, _):
            lanes = pl.ds(pl.multiple_of(j * LANES, LANES), LANES)
            y = buf[b, :, lanes] * inverse[src, j, pl.ds(e, 1), :]
            slots[s, lanes, :] = y.T.astype(jnp.bfloat16)
            return 0

        lax.fori_loop(0, tiles, tile, 0)
        out[src * experts + e, :, my_lanes] = slots[s, my_rows, :]
        if isinstance(e, int):
            if e + HELD < experts:
                load(src, e + HELD).start()
        else:
            @pl.when(e + HELD < experts)
            def _():
                load(src, e + HELD).start()

    def squares(x):
        return jnp.sum(x * x, axis=0, keepdims=True)

    def sums_held(src, e):
        load(src, e).wait()
        value = squares(buf[2 * e + src])
        if e == 0:
            part0[src] = value
        else:
            part1[src, e - 1:e, :] = value

    def sums_stream(begin, end):
        def one(e, _):
            for src in range(2):
                flow(src, e).wait()
                part2[src, pl.ds(e - HELD, 1), :] = squares(stream[(2 * (e - HELD) + src) % STREAM])

                @pl.when(e + STREAM // 2 < experts)
                def _():
                    flow(src, e + STREAM // 2).start()
            return 0
        lax.fori_loop(begin, end, one, 0)

    def keep(src, begin, end, total):
        scale = jnp.sqrt(total)
        scales[src, begin:end, :] = scale
        reciprocal = 1.0 / scale
        for j in range(tiles):
            inverse[src, j, begin:end, :] = reciprocal[:, j * LANES:(j + 1) * LANES]

    def greet(mask):
        return remote(part0, got0.at[mask - 1], send0.at[mask - 1], recv0.at[mask - 1],
                      {"shard": partner(me, n, mask)})

    def greet_end():
        for mask in range(1, n):
            greet(mask).wait()
        for src in range(2):
            total = part0[src]
            for mask in range(1, n):
                total = total + got0[mask - 1, src]
            keep(src, 0, 1, total)

    class Sums:
        def __init__(self, stages, begin, end, part, got, run, total, send, recv):
            self.stages, self.begin, self.end = stages, begin, end
            self.part, self.got, self.run, self.total = part, got, run, total
            self.send, self.recv = send, recv

        def copy(self, source, target, i, mask):
            return remote(source, target, self.send.at[i], self.recv.at[i],
                          {"shard": partner(me, n, mask)})

        def swap(self):
            return self.copy(self.part.at[1 - core], self.got.at[0], 0, 1)

        def swap_end(self):
            self.swap().wait()
            self.run[0] = self.part[core] + self.got[0]

        def passes(self, s):
            first = 1 + peers_of(self.stages[:s])
            return [self.copy(self.run.at[s], self.got.at[first + i], first + i, mask)
                    for i, mask in enumerate(self.stages[s])]

        def pass_start(self, s):
            for copy in self.passes(s):
                copy.start()

        def pass_end(self, s):
            value = self.run[s]
            for i, copy in enumerate(self.passes(s)):
                copy.wait()
                value = value + self.got[1 + peers_of(self.stages[:s]) + i]
            if s + 1 < len(self.stages):
                self.run[s + 1] = value
            else:
                self.total[core] = value

        def share(self):
            half = self.total.at[core]
            return self.copy(half, half, 1 + peers_of(self.stages), 1)

        def finish(self):
            self.share().wait()
            for src in range(2):
                keep(src, self.begin, self.end, self.total[src])

    early = Sums(EARLY, 1, HELD, part1, got1, run1, total1, send1, recv1)
    late = Sums(LATE, HELD, experts, part2, got2, run2, total2, send2, recv2)

    def mine(x):
        chosen = x[:, :narrow]
        for t in range(1, n):
            chosen = jnp.where(me == t, x[:, t * narrow:(t + 1) * narrow], chosen)
        return chosen

    def first_copy(mask):
        return remote(piece, column.at[:, my_lanes], first_send.at[mask - 1], first_recv.at[mask - 1],
                      {"shard": partner(me, n, mask)})

    my_columns = pl.ds(pl.multiple_of(mez * router_rows, router_rows), router_rows)

    def second_copy(r):
        return remote(column, router_out.at[my_columns, :], second_send.at[r - 1], second_recv.at[r - 1],
                      {"expert": lax.rem(mez + r, nz)})

    raw_units = [(src, mask) for group in OPENING for src, mask, raw in group if raw]

    def settle(src):
        row = 1.0 / mine(scales[src, 0:1, :])
        pad = -narrow % LANES
        if pad:
            row = jnp.concatenate([row, jnp.zeros((1, pad), jnp.float32)], axis=1)
        factor = jnp.broadcast_to(row, (LANES, narrow + pad)).T[:narrow]
        for which, mask in raw_units:
            if which != src:
                continue
            slab_copy(src, 0, mask, True).wait_recv()
            begin = partner(me, n, mask) * rows
            for j in range(rows // LANES):
                lanes = pl.ds(pl.multiple_of(begin + j * LANES, LANES), LANES)
                y = out[src * experts, :, lanes].astype(jnp.float32) * factor
                out[src * experts, :, lanes] = y.astype(jnp.bfloat16)

    last = len(PHASES)
    half = last // 2
    steps = experts - HELD
    cuts = [HELD + steps * i // 6 for i in range(7)]

    def chunk(i):
        sums_stream(cuts[i], cuts[i + 1])

    def run(k, begin, end):
        for q in range(begin, end):
            phase(k % 2, k // 2, q)

    def ahead(k):
        narrow_slab(k % 2, k // 2)

    sums_held(0, 0)
    sums_held(1, 0)
    raw_block(0, 6)
    pl.semaphore_wait(barrier, n - 1 + nz - 1)
    for mask in range(1, n):
        greet(mask).start()
    run(0, 0, 1)
    raw_block(0, 2)
    raw_block(1, 4)
    run(0, 1, 2)
    raw_block(1, 6)
    run(0, 2, 3)
    for e in range(1, HELD):
        for src in range(2):
            sums_held(src, e)
    early.swap().start()
    greet_end()
    ahead(0)
    run(0, 3, 4)
    run(1, 0, 1)
    early.swap_end()
    early.pass_start(0)
    ahead(1)
    run(1, 1, 2)
    weight_load.wait()
    gain_load.wait()
    value = (weight_in[...] * gain_in[...]).astype(jnp.bfloat16)
    piece[...] = value
    column[:, my_lanes] = value
    for mask in range(1, n):
        first_copy(mask).start()
    chunk(0)
    run(1, 2, 3)
    chunk(1)
    early.pass_end(0)
    early.share().start()
    run(1, 3, 4)
    chunk(2)
    early.finish()
    ahead(2)
    run(2, 0, 1)
    chunk(3)
    run(2, 1, 2)
    ahead(3)
    run(2, 2, 3)
    chunk(4)
    run(2, 3, 4)
    chunk(5)
    late.swap().start()
    run(3, 0, 1)
    late.swap_end()
    late.pass_start(0)
    run(3, 1, half)
    ahead(4)
    run(3, half, last)
    run(4, 0, half)
    late.pass_end(0)
    late.pass_start(1)
    ahead(5)
    run(4, half, last)
    run(5, 0, half)
    late.pass_end(1)
    late.share().start()
    ahead(6)
    run(5, half, last)
    late.finish()
    run(6, 0, half)
    ahead(7)
    for src in range(2):
        settle(src)
    run(6, half, last)
    for mask in range(1, n):
        first_copy(mask).wait()
    for r in range(1, nz):
        second_copy(r).start()
    router_out[my_columns, :] = column[...]
    run(7, 0, half)
    ahead(8)
    run(7, half, last)

    def step(e, _):
        for src in range(2):
            for q in range(half):
                phase(src, e, q)
            if src == 0:
                narrow_slab(1, e)
            else:
                @pl.when(e + 1 < experts)
                def _():
                    narrow_slab(0, e + 1)
            for q in range(half, last):
                phase(src, e, q)
        return 0

    lax.fori_loop(HELD, experts, step, 0)

    for ref, src in ((scale_gate, 0), (scale_up, 1)):
        ref[...] = mine(scales[src])
    for r in range(1, nz):
        second_copy(r).wait()
    for q in range(last - DEPTH, last):
        wait_phase(1, experts - 1, q)
    for mask in range(1, n):
        for src in range(2):
            begin = src * experts + (1 if (src, mask) in raw_units else 0)
            whole = out.at[begin:(src + 1) * experts, :, my_lanes]
            remote(whole, whole, send_sem.at[0, mask - 1], recv_sem.at[src, mask - 1],
                   {"shard": partner(me, n, mask)}).wait_recv()


def deliver(experts, out, scale_gate, scale_up, router,
            to_gate, to_up, to_scale_gate, to_scale_up, to_router, sem):
    copies = [
        pltpu.make_async_copy(source, target, sem.at[i])
        for i, (source, target) in enumerate((
            (out.at[:experts], to_gate), (out.at[experts:], to_up),
            (scale_gate, to_scale_gate), (scale_up, to_scale_up), (router, to_router)))
    ]
    for copy in copies:
        copy.start()
    for copy in copies:
        copy.wait()


def fused(n, nz, master_gate, master_up, router_weight, router_gain):
    experts, rows, width = master_gate.shape
    slabs = 2 * experts
    narrow = width // n
    router_rows = router_weight.shape[1]
    vmem = pl.BlockSpec(memory_space=pltpu.VMEM)
    hbm = pl.BlockSpec(memory_space=pltpu.HBM)
    dma = pltpu.SemaphoreType.DMA
    f32, bf16 = jnp.float32, jnp.bfloat16

    def sums(count, stages):
        peers = peers_of(stages)
        return [
            pltpu.VMEM((2, count, width), f32),
            pltpu.VMEM((1 + peers, count, width), f32),
            pltpu.VMEM((len(stages), count, width), f32),
            pltpu.VMEM((2, count, width), f32),
        ]

    results = pl.pallas_call(
        functools.partial(kernel, n, nz),
        out_shape=(
            pltpu.VMEM((slabs, narrow, rows * n), bf16),
            pltpu.VMEM((experts, narrow), f32),
            pltpu.VMEM((experts, narrow), f32),
            pltpu.VMEM((router_rows * nz, rows * n), bf16),
        ),
        in_specs=[hbm] * 4,
        out_specs=(vmem,) * 4,
        scratch_shapes=[
            pltpu.VMEM((2 * HELD, rows, width), f32),
            pltpu.VMEM((STREAM, rows, width), f32),
            pltpu.VMEM((SLOTS, width, rows), bf16),
            pltpu.VMEM((2, 1, width), f32),
            pltpu.VMEM((n - 1, 2, 1, width), f32),
            *sums(HELD - 1, EARLY),
            *sums(experts - HELD, LATE),
            pltpu.VMEM((2, experts, width), f32),
            pltpu.VMEM((2, width // LANES, experts, LANES), f32),
            pltpu.VMEM((router_rows, rows), f32),
            pltpu.VMEM((1, rows), f32),
            pltpu.VMEM((router_rows, rows), bf16),
            pltpu.VMEM((router_rows, rows * n), bf16),
            dma((2 * HELD,)), dma((STREAM,)), dma((2,)),
            dma((SLOTS, n - 1)), dma((2, n - 1)), dma((2, n - 1)),
            dma((n - 1,)), dma((n - 1,)),
            dma((2 + peers_of(EARLY),)), dma((2 + peers_of(EARLY),)),
            dma((2 + peers_of(LATE),)), dma((2 + peers_of(LATE),)),
            dma((n - 1,)), dma((n - 1,)), dma((nz - 1,)), dma((nz - 1,)),
        ],
        compiler_params=pltpu.CompilerParams(
            collective_id=0, has_side_effects=True,
            vmem_limit_bytes=VMEM_LIMIT - slabs * narrow * rows * n * 2 - SPARE),
        name="exchange",
    )(master_gate, master_up, router_weight.T, router_gain[None, :])
    final_gate, final_up, scale_gate, scale_up, router = pl.pallas_call(
        functools.partial(deliver, experts),
        out_shape=(
            jax.ShapeDtypeStruct((experts, narrow, rows * n), bf16),
            jax.ShapeDtypeStruct((experts, narrow, rows * n), bf16),
            jax.ShapeDtypeStruct((experts, narrow), f32),
            jax.ShapeDtypeStruct((experts, narrow), f32),
            jax.ShapeDtypeStruct((router_rows * nz, rows * n), bf16),
        ),
        in_specs=[vmem] * 4,
        out_specs=(hbm,) * 5,
        scratch_shapes=[dma((5,))],
        compiler_params=pltpu.CompilerParams(vmem_limit_bytes=1048576),
        name="deliver",
    )(*(pltpu.with_memory_space_constraint(x, pltpu.VMEM) for x in results))
    return (final_gate.swapaxes(1, 2), final_up.swapaxes(1, 2), scale_gate, scale_up, router.T)


def solution(mesh):
    n, nz = mesh.shape["shard"], mesh.shape["expert"]

    def local(master_gate, master_up, router_weight, router_gain):
        experts, rows, width = master_gate.shape
        slabs = 2 * experts
        held = (
            (2 * HELD + STREAM) * rows * width * 4 + SLOTS * rows * width * 2
            + slabs * rows * width * 2 + 16 * slabs * width * 4
        )
        fits = (
            n == 8 and nz > 1 and held <= VMEM_LIMIT - 2 * SPARE
            and rows % LANES == 0 and width % LANES == 0 and width % (16 * n) == 0
            and experts >= HELD + 6 and router_weight.shape[1] % 16 == 0
        )
        if not fits:
            return plain(master_gate, master_up, router_weight, router_gain)
        return fused(n, nz, master_gate, master_up, router_weight, router_gain)

    in_specs = (
        P("expert", "shard", None),
        P("expert", "shard", None),
        P("shard", "expert"),
        P("shard"),
    )
    out_specs = (
        P("expert", None, "shard"),
        P("expert", None, "shard"),
        P("expert", "shard"),
        P("expert", "shard"),
        P(),
    )
    return jax.shard_map(local, mesh=mesh, in_specs=in_specs, out_specs=out_specs, check_vma=False)
```

time: 278 us -> 271 us (0.975)
  Pallas kernels: 277 us -> 270 us
    pallas_call x1, Pallas kernels: 269 us -> 262 us  [fused(): pl.pallas_call(functools.partial(kernel, n, nz), out_shape=(pltpu.VMEM((s...]
where the time goes in v2:
time: 271 us
  Pallas kernels  270 us (100%)
    pallas_call x1, Pallas kernels, fused(): pl.pallas_call(functools.partial(kernel, n, nz), out_shape=(pltpu.VMEM((s...  262 us
    pallas_call x1, Pallas kernels, fused(): pl.pallas_call(functools.partial(deliver, experts), out_shape=(jax.ShapeD...  8.28 us

profile of v2, /device:TPU:1, one launch (start us, length us, event | category | flops | bytes accessed | tf_op | source)
XLA Modules:
  0.0 270.5 jit_solution(12878223024087722516)
XLA Ops:
  0.6 261.6 %exchange.1 = (bf16[32,176,2048]{2,1,0:T(8,128)(2,1)S(1)}, f32[16,176]{1,0:T(8,128)S(1)}, f32[16,176]{1,0:T(8,128)S(1)}, bf16[64,2048]{1,0:T(8,128)(2,1)S(1)}) custom-call(f32[16,256,1408]{2,1,0:T(8,128)} %gate.1, f32[16,256,1408]{2,1,0:T(8,128)} %up.1, f32[16,256]{1,0:T(8,128)} %bitcast.5, f32[1,256]{1,0:T(1,128)} %bitcast.6), custom_call_target="tpu_custom_call" | custom-call | tf_op jit(solution)/shard_map/exchange/pallas_call | solution.py:467
  262.2 8.3 %deliver.1 = (bf16[16,176,2048]{2,1,0:T(8,128)(2,1)}, bf16[16,176,2048]{2,1,0:T(8,128)(2,1)}, f32[16,176]{1,0:T(8,128)}, f32[16,176]{1,0:T(8,128)}, bf16[64,2048]{1,0:T(8,128)(2,1)}) custom-call(bf16[32,176,2048]{2,1,0:T(8,128)(2,1)S(1)} %get-tuple-element.14.out, f32[16,176]{1,0:T(8,128)S(1)} %get-tuple-element.15.scale_gate, ...), custom_call_target="tpu_custom_call" | custom-call | tf_op jit(solution)/shard_map/deliver/pallas_call | solution.py:503

commit v3 on v2

--- a/solution.py
+++ b/solution.py
@@ -79,7 +79,7 @@
            scales, inverse, weight_in, gain_in, piece, column,
            load_sem, stream_sem, router_sem, send_sem, recv_sem, raw_sem,
            send0, recv0, send1, recv1, send2, recv2,
-           first_send, first_recv, second_send, second_recv):
+           first_send, first_recv, second_send, second_recv, third_send, third_recv, go):
     me = lax.axis_index("shard")
     mez = lax.axis_index("expert")
     core = lax.rem(me, 2)
@@ -110,12 +110,28 @@
             flow(src, e).start()
 
     barrier = pltpu.get_barrier_semaphore()
-    for mask in range(1, n):
-        pl.semaphore_signal(barrier, inc=1, device_id={"shard": partner(me, n, mask)},
+    for chip in range(n // 2):
+        @pl.when(me != 2 * chip)
+        def _():
+            pl.semaphore_signal(barrier, inc=1, device_id={"shard": 2 * chip},
+                                device_id_type=pl.DeviceIdType.MESH)
+
+    @pl.when(core == 1)
+    def _():
+        for r in range(1, nz):
+            pl.semaphore_signal(barrier, inc=1, device_id={"expert": lax.rem(mez + r, nz)},
+                                device_id_type=pl.DeviceIdType.MESH)
+
+    @pl.when(core == 0)
+    def _():
+        pl.semaphore_wait(barrier, n - 1)
+        pl.semaphore_signal(go, inc=1, device_id={"shard": partner(me, n, 1)},
                             device_id_type=pl.DeviceIdType.MESH)
-    for r in range(1, nz):
-        pl.semaphore_signal(barrier, inc=1, device_id={"expert": lax.rem(mez + r, nz)},
-                            device_id_type=pl.DeviceIdType.MESH)
+
+    def greeted():
+        @pl.when(core == 1)
+        def _():
+            pl.semaphore_wait(go, 1)
 
     my_lanes = pl.ds(pl.multiple_of(me * rows, rows), rows)
     my_rows = pl.ds(pl.multiple_of(me * narrow, 16), narrow)
@@ -171,7 +187,7 @@
             slots[s, lanes, :] = y.T.astype(jnp.bfloat16)
             return 0
 
-        lax.fori_loop(0, tiles, tile, 0)
+        lax.fori_loop(0, tiles, tile, 0, unroll=True)
         out[src * experts + e, :, my_lanes] = slots[s, my_rows, :]
         if isinstance(e, int):
             if e + HELD < experts:
@@ -287,6 +303,11 @@
     def second_copy(r):
         return remote(column, router_out.at[my_columns, :], second_send.at[r - 1], second_recv.at[r - 1],
                       {"expert": lax.rem(mez + r, nz)})
+
+    def third_copy(r):
+        theirs = pl.ds(pl.multiple_of(lax.rem(mez + r, nz) * router_rows, router_rows), router_rows)
+        return remote(router_out.at[theirs, :], router_out.at[theirs, :],
+                      third_send.at[r - 1], third_recv.at[r - 1], {"shard": partner(me, n, 1)})
 
     raw_units = [(src, mask) for group in OPENING for src, mask, raw in group if raw]
 
@@ -324,7 +345,7 @@
     sums_held(0, 0)
     sums_held(1, 0)
     raw_block(0, 6)
-    pl.semaphore_wait(barrier, n - 1 + nz - 1)
+    greeted()
     for mask in range(1, n):
         greet(mask).start()
     run(0, 0, 1)
@@ -339,10 +360,10 @@
     early.swap().start()
     greet_end()
     ahead(0)
+    early.swap_end()
+    early.pass_start(0)
     run(0, 3, 4)
     run(1, 0, 1)
-    early.swap_end()
-    early.pass_start(0)
     ahead(1)
     run(1, 1, 2)
     weight_load.wait()
@@ -358,10 +379,10 @@
     early.pass_end(0)
     early.share().start()
     run(1, 3, 4)
-    chunk(2)
     early.finish()
     ahead(2)
     run(2, 0, 1)
+    chunk(2)
     chunk(3)
     run(2, 1, 2)
     ahead(3)
@@ -394,12 +415,36 @@
     run(6, half, last)
     for mask in range(1, n):
         first_copy(mask).wait()
-    for r in range(1, nz):
-        second_copy(r).start()
     router_out[my_columns, :] = column[...]
+
+    @pl.when(core == 1)
+    def _():
+        pl.semaphore_wait(barrier, nz - 1)
+        for r in range(1, nz):
+            second_copy(r).start()
+
     run(7, 0, half)
     ahead(8)
     run(7, half, last)
+
+    @pl.when(core == 1)
+    def _():
+        for r in range(1, nz):
+            second_copy(r).wait()
+        for r in range(1, nz):
+            third_copy(r).start()
+
+    run(8, 0, half)
+    ahead(9)
+    run(8, half, last)
+    run(9, 0, half)
+    ahead(10)
+    run(9, half, last)
+
+    @pl.when(core == 1)
+    def _():
+        for r in range(1, nz):
+            third_copy(r).wait_send()
 
     def step(e, _):
         for src in range(2):
@@ -415,14 +460,18 @@
                 phase(src, e, q)
         return 0
 
-    lax.fori_loop(HELD, experts, step, 0)
+    lax.fori_loop(HELD + 1, experts, step, 0)
 
     for ref, src in ((scale_gate, 0), (scale_up, 1)):
         ref[...] = mine(scales[src])
-    for r in range(1, nz):
-        second_copy(r).wait()
-    for q in range(last - DEPTH, last):
-        wait_phase(1, experts - 1, q)
+
+    @pl.when(core == 0)
+    def _():
+        for r in range(1, nz):
+            third_copy(r).wait_recv()
+
+    for q in range(2 * last - DEPTH, 2 * last):
+        wait_phase(q // last, experts - 1, q % last)
     for mask in range(1, n):
         for src in range(2):
             begin = src * experts + (1 if (src, mask) in raw_units else 0)
@@ -433,12 +482,10 @@
 
 def deliver(experts, out, scale_gate, scale_up, router,
             to_gate, to_up, to_scale_gate, to_scale_up, to_router, sem):
-    copies = [
-        pltpu.make_async_copy(source, target, sem.at[i])
-        for i, (source, target) in enumerate((
-            (out.at[:experts], to_gate), (out.at[experts:], to_up),
-            (scale_gate, to_scale_gate), (scale_up, to_scale_up), (router, to_router)))
-    ]
+    pairs = [(scale_gate, to_scale_gate), (scale_up, to_scale_up), (router, to_router)]
+    for e in range(experts):
+        pairs += [(out.at[e], to_gate.at[e]), (out.at[experts + e], to_up.at[e])]
+    copies = [pltpu.make_async_copy(a, b, sem.at[i]) for i, (a, b) in enumerate(pairs)]
     for copy in copies:
         copy.start()
     for copy in copies:
@@ -494,6 +541,7 @@
             dma((2 + peers_of(EARLY),)), dma((2 + peers_of(EARLY),)),
             dma((2 + peers_of(LATE),)), dma((2 + peers_of(LATE),)),
             dma((n - 1,)), dma((n - 1,)), dma((nz - 1,)), dma((nz - 1,)),
+            dma((nz - 1,)), dma((nz - 1,)), pltpu.SemaphoreType.REGULAR,
         ],
         compiler_params=pltpu.CompilerParams(
             collective_id=0, has_side_effects=True,
@@ -511,7 +559,7 @@
         ),
         in_specs=[vmem] * 4,
         out_specs=(hbm,) * 5,
-        scratch_shapes=[dma((5,))],
+        scratch_shapes=[dma((2 * experts + 3,))],
         compiler_params=pltpu.CompilerParams(vmem_limit_bytes=1048576),
         name="deliver",
     )(*(pltpu.with_memory_space_constraint(x, pltpu.VMEM) for x in results))

time: 271 us -> 268 us (0.989)
  Pallas kernels: 270 us -> 267 us
where the time goes in v3:
time: 268 us
  Pallas kernels  267 us (100%)
    pallas_call x1, Pallas kernels, fused(): pl.pallas_call(functools.partial(kernel, n, nz), out_shape=(pltpu.VMEM((s...  259 us
    pallas_call x1, Pallas kernels, fused(): pl.pallas_call(functools.partial(deliver, experts), out_shape=(jax.ShapeD...  8.1 us

profile of v3, /device:TPU:1, one launch (start us, length us, event | category | flops | bytes accessed | tf_op | source)
XLA Modules:
  0.0 267.7 jit_solution(15553011984900030504)
XLA Ops:
  0.6 258.9 %exchange.1 = (bf16[32,176,2048]{2,1,0:T(8,128)(2,1)S(1)}, f32[16,176]{1,0:T(8,128)S(1)}, f32[16,176]{1,0:T(8,128)S(1)}, bf16[64,2048]{1,0:T(8,128)(2,1)S(1)}) custom-call(f32[16,256,1408]{2,1,0:T(8,128)} %gate.1, f32[16,256,1408]{2,1,0:T(8,128)} %up.1, f32[16,256]{1,0:T(8,128)} %bitcast.5, f32[1,256]{1,0:T(1,128)} %bitcast.6), custom_call_target="tpu_custom_call" | custom-call | tf_op jit(solution)/shard_map/exchange/pallas_call | solution.py:514
  259.6 8.1 %deliver.1 = (bf16[16,176,2048]{2,1,0:T(8,128)(2,1)}, bf16[16,176,2048]{2,1,0:T(8,128)(2,1)}, f32[16,176]{1,0:T(8,128)}, f32[16,176]{1,0:T(8,128)}, bf16[64,2048]{1,0:T(8,128)(2,1)}) custom-call(bf16[32,176,2048]{2,1,0:T(8,128)(2,1)S(1)} %get-tuple-element.14.out, f32[16,176]{1,0:T(8,128)S(1)} %get-tuple-element.15.scale_gate, ...), custom_call_target="tpu_custom_call" | custom-call | tf_op jit(solution)/shard_map/deliver/pallas_call | solution.py:551

commit v4 on v3

--- a/solution.py
+++ b/solution.py
@@ -13,16 +13,6 @@
 SLOTS = 4
 DEPTH = 3
 PHASES = ((6, 1), (2, 4), (7,), (3, 5))
-OPENING = (
-    ((0, 6, True),),
-    ((0, 2, True), (1, 4, True)),
-    ((1, 6, True),),
-    ((0, 7, False), (0, 1, False)),
-    ((0, 3, False), (0, 4, False)),
-    ((1, 7, False), (1, 1, False)),
-    ((1, 2, False), (1, 5, False)),
-    ((1, 3, False), (0, 5, False)),
-)
 EARLY = ((2, 4, 6),)
 LATE = ((2,), (4,))
 VMEM_LIMIT = 67043328
@@ -64,6 +54,10 @@
     return index
 
 
+def raw_rows_of(narrow, experts):
+    return narrow * experts // 61 // 16 * 16
+
+
 def peers_of(stages):
     return sum(len(stage) for stage in stages)
 
@@ -77,7 +71,7 @@
 def kernel(n, nz, gate, up, weight, gain, out, scale_gate, scale_up, router_out,
            buf, stream, slots, part0, got0, part1, got1, run1, total1, part2, got2, run2, total2,
            scales, inverse, weight_in, gain_in, piece, column,
-           load_sem, stream_sem, router_sem, send_sem, recv_sem, raw_sem,
+           load_sem, stream_sem, router_sem, send_sem, recv_sem, raw_sem, rest_sem,
            send0, recv0, send1, recv1, send2, recv2,
            first_send, first_recv, second_send, second_recv, third_send, third_recv, go):
     me = lax.axis_index("shard")
@@ -85,6 +79,7 @@
     core = lax.rem(me, 2)
     experts, rows, width = gate.shape
     narrow = width // n
+    raw_rows = raw_rows_of(narrow, experts)
     tiles = width // LANES
     router_rows = weight.shape[0]
     sources = (gate, up)
@@ -136,44 +131,54 @@
     my_lanes = pl.ds(pl.multiple_of(me * rows, rows), rows)
     my_rows = pl.ds(pl.multiple_of(me * narrow, 16), narrow)
 
-    def slab_copy(src, e, mask, raw):
-        s = 2 + src if raw else (2 * e + src) % SLOTS
+    def slab_copy(src, e, mask, raw=False):
+        s = (2 * e + src) % SLOTS
         target = partner(me, n, mask)
+        begin, count = target * narrow, narrow
+        first = isinstance(e, int) and e == 0
+        sem = recv_sem
+        if raw:
+            s, count, sem = 2 + src, raw_rows, raw_sem
+        elif first:
+            sem = rest_sem
+            if mask > 1:
+                begin, count = begin + raw_rows, narrow - raw_rows
         return remote(
-            slots.at[s, pl.ds(pl.multiple_of(target * narrow, 16), narrow), :],
-            out.at[src * experts + e, :, my_lanes],
-            send_sem.at[s, mask - 1], (raw_sem if raw else recv_sem).at[src, mask - 1],
-            {"shard": target})
-
-    def units(src, e, q):
-        if isinstance(e, int) and e == 0:
-            return OPENING[len(PHASES) * src + q]
-        return [(src, mask, False) for mask in PHASES[q]]
+            slots.at[s, pl.ds(pl.multiple_of(begin, 16), count), :],
+            out.at[src * experts + e, narrow - count if first and not raw else 0:count if raw else narrow, my_lanes]
+            if first else out.at[src * experts + e, :, my_lanes],
+            send_sem.at[s, mask - 1], sem.at[src, mask - 1], {"shard": target})
+
+    def raw_slab(src):
+        def tile(j, _):
+            lanes = pl.ds(pl.multiple_of(j * LANES, LANES), LANES)
+            slots[2 + src, lanes, :] = buf[src, :, lanes].T.astype(jnp.bfloat16)
+            return 0
+
+        lax.fori_loop(0, tiles, tile, 0, unroll=True)
+
+    def raw_send(src):
+        for mask in range(2, n):
+            slab_copy(src, 0, mask, True).start()
 
     def wait_phase(src, e, q):
-        for which, mask, raw in units(src, e, q):
-            slab_copy(which, e, mask, raw).wait_send()
+        if isinstance(e, int) and e < 0:
+            raw = len(PHASES) * (2 * e + src) + q + 2
+            if raw >= 0:
+                for mask in range(2, n):
+                    slab_copy(raw, 0, mask, True).wait_send()
+            return
+        for mask in PHASES[q]:
+            slab_copy(src, e, mask).wait_send()
 
     def phase(src, e, q):
         back, before = q - DEPTH, src
         while back < 0:
             back += len(PHASES)
             before -= 1
-        lag = e + before // 2
-        if not isinstance(lag, int) or lag >= 0:
-            wait_phase(before % 2, lag, back)
-        for which, mask, raw in units(src, e, q):
-            slab_copy(which, e, mask, raw).start()
-
-    def raw_block(src, mask):
-        begin = partner(me, n, mask) * narrow
-
-        def tile(j, _):
-            lanes = pl.ds(pl.multiple_of(j * LANES, LANES), LANES)
-            slots[2 + src, lanes, :] = buf[src, :, lanes].T.astype(jnp.bfloat16)
-            return 0
-
-        lax.fori_loop(begin // LANES, (begin + narrow - 1) // LANES + 1, tile, 0)
+        wait_phase(before % 2, e + before // 2, back)
+        for mask in PHASES[q]:
+            slab_copy(src, e, mask).start()
 
     def narrow_slab(src, e):
         k = 2 * e + src
@@ -309,23 +314,19 @@
         return remote(router_out.at[theirs, :], router_out.at[theirs, :],
                       third_send.at[r - 1], third_recv.at[r - 1], {"shard": partner(me, n, 1)})
 
-    raw_units = [(src, mask) for group in OPENING for src, mask, raw in group if raw]
-
     def settle(src):
         row = 1.0 / mine(scales[src, 0:1, :])
         pad = -narrow % LANES
         if pad:
             row = jnp.concatenate([row, jnp.zeros((1, pad), jnp.float32)], axis=1)
-        factor = jnp.broadcast_to(row, (LANES, narrow + pad)).T[:narrow]
-        for which, mask in raw_units:
-            if which != src:
-                continue
+        factor = jnp.broadcast_to(row, (LANES, narrow + pad)).T[:raw_rows]
+        for mask in range(2, n):
             slab_copy(src, 0, mask, True).wait_recv()
             begin = partner(me, n, mask) * rows
             for j in range(rows // LANES):
                 lanes = pl.ds(pl.multiple_of(begin + j * LANES, LANES), LANES)
-                y = out[src * experts, :, lanes].astype(jnp.float32) * factor
-                out[src * experts, :, lanes] = y.astype(jnp.bfloat16)
+                y = out[src * experts, :raw_rows, lanes].astype(jnp.float32) * factor
+                out[src * experts, :raw_rows, lanes] = y.astype(jnp.bfloat16)
 
     last = len(PHASES)
     half = last // 2
@@ -344,28 +345,25 @@
 
     sums_held(0, 0)
     sums_held(1, 0)
-    raw_block(0, 6)
+    raw_slab(0)
     greeted()
     for mask in range(1, n):
         greet(mask).start()
-    run(0, 0, 1)
-    raw_block(0, 2)
-    raw_block(1, 4)
-    run(0, 1, 2)
-    raw_block(1, 6)
-    run(0, 2, 3)
+    raw_send(0)
+    raw_slab(1)
+    raw_send(1)
     for e in range(1, HELD):
         for src in range(2):
             sums_held(src, e)
     early.swap().start()
     greet_end()
     ahead(0)
+    run(0, 0, 1)
     early.swap_end()
     early.pass_start(0)
-    run(0, 3, 4)
-    run(1, 0, 1)
+    run(0, 1, 4)
     ahead(1)
-    run(1, 1, 2)
+    run(1, 0, 2)
     weight_load.wait()
     gain_load.wait()
     value = (weight_in[...] * gain_in[...]).astype(jnp.bfloat16)
@@ -474,8 +472,8 @@
         wait_phase(q // last, experts - 1, q % last)
     for mask in range(1, n):
         for src in range(2):
-            begin = src * experts + (1 if (src, mask) in raw_units else 0)
-            whole = out.at[begin:(src + 1) * experts, :, my_lanes]
+            slab_copy(src, 0, mask).wait_recv()
+            whole = out.at[src * experts + 1:(src + 1) * experts, :, my_lanes]
             remote(whole, whole, send_sem.at[0, mask - 1], recv_sem.at[src, mask - 1],
                    {"shard": partner(me, n, mask)}).wait_recv()
 
@@ -536,7 +534,7 @@
             pltpu.VMEM((router_rows, rows), bf16),
             pltpu.VMEM((router_rows, rows * n), bf16),
             dma((2 * HELD,)), dma((STREAM,)), dma((2,)),
-            dma((SLOTS, n - 1)), dma((2, n - 1)), dma((2, n - 1)),
+            dma((SLOTS, n - 1)), dma((2, n - 1)), dma((2, n - 1)), dma((2, n - 1)),
             dma((n - 1,)), dma((n - 1,)),
             dma((2 + peers_of(EARLY),)), dma((2 + peers_of(EARLY),)),
             dma((2 + peers_of(LATE),)), dma((2 + peers_of(LATE),)),
@@ -579,7 +577,7 @@
         fits = (
             n == 8 and nz > 1 and held <= VMEM_LIMIT - 2 * SPARE
             and rows % LANES == 0 and width % LANES == 0 and width % (16 * n) == 0
-            and experts >= HELD + 6 and router_weight.shape[1] % 16 == 0
+            and experts >= HELD + 6 and raw_rows_of(width // n, experts) > 0 and router_weight.shape[1] % 16 == 0
         )
         if not fits:
             return plain(master_gate, master_up, router_weight, router_gain)

time: 268 us -> 269 us (level)
  no operation moved by 1% of the time
where the time goes in v4:
time: 269 us
  Pallas kernels  268 us (100%)
    pallas_call x1, Pallas kernels, fused(): pl.pallas_call(functools.partial(kernel, n, nz), out_shape=(pltpu.VMEM((s...  260 us
    pallas_call x1, Pallas kernels, fused(): pl.pallas_call(functools.partial(deliver, experts), out_shape=(jax.ShapeD...  8.1 us

profile of v4, /device:TPU:1, one launch (start us, length us, event | category | flops | bytes accessed | tf_op | source)
XLA Modules:
  0.0 268.9 jit_solution(4724306910222242802)
XLA Ops:
  0.6 260.2 %exchange.1 = (bf16[32,176,2048]{2,1,0:T(8,128)(2,1)S(1)}, f32[16,176]{1,0:T(8,128)S(1)}, f32[16,176]{1,0:T(8,128)S(1)}, bf16[64,2048]{1,0:T(8,128)(2,1)S(1)}) custom-call(f32[16,256,1408]{2,1,0:T(8,128)} %gate.1, f32[16,256,1408]{2,1,0:T(8,128)} %up.1, f32[16,256]{1,0:T(8,128)} %bitcast.5, f32[1,256]{1,0:T(1,128)} %bitcast.6), custom_call_target="tpu_custom_call" | custom-call | tf_op jit(solution)/shard_map/exchange/pallas_call | solution.py:512
  260.8 8.1 %deliver.1 = (bf16[16,176,2048]{2,1,0:T(8,128)(2,1)}, bf16[16,176,2048]{2,1,0:T(8,128)(2,1)}, f32[16,176]{1,0:T(8,128)}, f32[16,176]{1,0:T(8,128)}, bf16[64,2048]{1,0:T(8,128)(2,1)}) custom-call(bf16[32,176,2048]{2,1,0:T(8,128)(2,1)S(1)} %get-tuple-element.14.out, f32[16,176]{1,0:T(8,128)S(1)} %get-tuple-element.15.scale_gate, ...), custom_call_target="tpu_custom_call" | custom-call | tf_op jit(solution)/shard_map/deliver/pallas_call | solution.py:549
